TPU v7x, 32 devices: a whole 2x2x4 slice. The times are simulated.
32 devices in a mesh: row: 4 (over z), col: 8 (over y, x, core).
Axes of the slice: x: 2, y: 2, z: 4, core: 2. Of those that a mesh axis runs over, the one named last changes fastest.
Arguments:
- coefs: float32 [2, 384, 16384], P(None, 'row', 'col'), may hold values from -600 to 600, as said below
- tilts: int32 [384, 2], replicated, may hold values from 8 to 48
- start_basis: float32 [384, 32], P('col'), may hold values from -6 to 6
Outputs:
- ccc: float32 [384, 384], P('row', 'col')
- basis: float32 [384, 32], P('col')
Inputs may be any that keep to these rules, and one draw needn't show every extreme that they name: `coefs`: real and imaginary parts are products of a particle scale, a coefficient scale and a bounded random value.
All inputs are finite; a program needn't handle non-finite values.
Results may differ from a plain program's by a relative error of at most 0.0003.
Values sent between devices are 32-bit elements; how exact they have to be, the bound alone decides.
A program may use at most 192 MiB of HBM per device.

v0:
```python
import math
import jax
import jax.numpy as jnp
from jax import lax
from jax.sharding import PartitionSpec as P

GRID = 32
ITERS = 4
EPS = 1e-06
HIGH = lax.Precision.HIGHEST


def wedge(tilt_rows, wave_index):
    wave_x = jnp.abs(wave_index // (GRID * (GRID // 2)) - GRID // 2)[None, :]
    wave_z = (wave_index % GRID - GRID // 2)[None, :]
    upward = wave_z * 16 <= tilt_rows[:, 1:2] * wave_x
    downward = -wave_z * 16 <= tilt_rows[:, 0:1] * wave_x
    return jnp.where(wave_z >= 0, upward, downward).astype(jnp.float32)


def inner(left, right):
    return lax.dot_general(
        left, right, (((1,), (1,)), ((), ())), precision=HIGH, preferred_element_type=jnp.float32
    )


def prepare(values, tilt_rows, wave_index):
    masks = wedge(tilt_rows, wave_index)
    paired = jnp.concatenate([values[0] * masks, values[1] * masks], axis=1)
    energy = masks * (values[0] * values[0] + values[1] * values[1])
    return (masks, paired, energy)


def local(coefs, tilts, start_basis):
    row_count = coefs.shape[1]
    slice_width = coefs.shape[2]
    col_count = start_basis.shape[0]
    col_size = lax.axis_size("col")
    total = col_count * col_size
    row_index = lax.axis_index("row")
    col_index = lax.axis_index("col")
    own_tilts = lax.dynamic_slice_in_dim(tilts, row_index * row_count, row_count, 0)
    wave_index = col_index * slice_width + jnp.arange(slice_width, dtype=jnp.int32)
    own_mask, own_pair, own_energy = prepare(coefs, own_tilts, wave_index)
    gathered = lax.all_gather(coefs, "row", axis=1, tiled=True)
    mask_j, pair_j, energy_j = prepare(gathered, tilts, wave_index)
    numer = inner(pair_j, own_pair)
    first = inner(mask_j, own_energy)
    second = inner(energy_j, own_mask)
    summed = lax.psum_scatter(
        jnp.concatenate([numer, first, second], axis=1), "col", scatter_dimension=0, tiled=True
    )
    numer = summed[:, :row_count]
    first = summed[:, row_count : 2 * row_count]
    second = summed[:, 2 * row_count :]
    block = (numer / jnp.sqrt(first * second + EPS)).T
    current = start_basis
    for step in range(ITERS):
        partial_value = jnp.dot(block, current, precision=HIGH, preferred_element_type=jnp.float32)
        summed_rows = lax.psum(partial_value, "col")
        local_gram = lax.dot_general(
            summed_rows,
            summed_rows,
            (((0,), (0,)), ((), ())),
            precision=HIGH,
            preferred_element_type=jnp.float32,
        )
        gram = lax.psum(local_gram, "row")
        factor = jnp.linalg.cholesky(gram)
        fresh = lax.linalg.triangular_solve(
            factor, summed_rows, left_side=False, lower=True, transpose_a=True
        )
        whole = lax.all_gather(fresh, "row", axis=0, tiled=True)
        current = lax.dynamic_slice_in_dim(whole, col_index * col_count, col_count, 0)
    return (block, current * math.sqrt(total))


def solution(mesh):
    in_specs = (P(None, "row", "col"), P(), P("col", None))
    out_specs = (P("row", "col"), P("col", None))
    return jax.shard_map(local, mesh=mesh, in_specs=in_specs, out_specs=out_specs, check_vma=False)
```

profile of v0, /device:TPU:0, one launch (start us, length us, event | category | flops | bytes accessed | tf_op | source)
XLA Modules:
  0.0 422.8 jit_solution(8679208534305008273)
XLA Ops:
  7.2 0.7 all-gather.6.cloned.1.call-update
  8.0 0.8 constant_dynamic-slice_fusion
  8.8 0.8 slice_reduce_fusion.1
  9.6 4.0 fusion.18
  13.6 0.4 bitcast_select_fusion.1
  14.0 113.6 %all-gather.6.cloned.1.call-done = f32[2,384,2048]{2,1,0:T(8,128)} async-done(((f32[2,96,2048]{2,1,0:T(8,128)}), f32[2,384,2048]{2,1,0:T(8,128)}) %all-gather.6.cloned.1.call-update) | async-done | bytes 6291472 | tf_op jit(solution)/shard_map/all_gather | solution.py:45
  127.6 4.1 fusion.10
  131.8 6.0 %fusion = f32[384,96]{0,1:T(8,128)S(1)} fusion(f32[384,2048]{1,0:T(8,128)S(1)} %get-tuple-element.13, f32[384,2048]{1,0:T(8,128)S(1)} %get-tuple-element.12, f32[96,2048]{1,0:T(8,128)S(1)} %get-tuple-element.15, f32[96,2048]{1,0:T(8,128)S(1)} %get-tuple-element.14), kind=kOutput, calls=%fused_computation | convolution fusion | flops 1813905408 | bytes 8011776 | tf_op jit(solution)/shard_map/dot_general | solution.py:22
  137.8 3.2 fusion.4
  141.1 1.2 copy.44
  142.3 32.7 %reduce-scatter.4.cloned.1.call-done = f32[48,288]{1,0:T(8,128)} async-done(((f32[384,288]{1,0:T(8,128)}), f32[48,288]{1,0:T(8,128)}) %reduce-scatter.4.cloned.1.call-update) | async-done | bytes 55312
  175.0 0.9 fusion.67
  176.5 22.5 %psum.56 = f32[96,32]{0,1:T(8,128)S(1)} all-reduce(f32[96,32]{0,1:T(8,128)S(1)} %fusion.68), channel_id=1, replica_groups=mesh['row'=4,'col'=8] {'col'}, use_global_device_ids=true, to_apply=%region_1.2 | all-reduce | flops 3072 | bytes 24576 | tf_op jit(solution)/shard_map/psum | solution.py:60
  199.2 18.7 %psum.57 = f32[32,32]{0,1:T(8,128)S(1)} all-reduce(f32[32,32]{0,1:T(8,128)S(1)} %fusion.69), channel_id=1, replica_groups=mesh['row'=4,'col'=8] {'row'}, use_global_device_ids=true, to_apply=%region_2.3 | all-reduce | flops 1024 | bytes 8192 | tf_op jit(solution)/shard_map/psum | solution.py:68
  218.0 2.9 cholesky.74
  220.9 0.6 compare_reduce_fusion.3
  221.6 0.7 fusion.24
  222.2 2.4 custom-call.8
  224.6 0.2 convolution_bitcast_fusion.3
  224.9 0.7 copy.39
  225.6 13.1 %all-gather = f32[4,96,32]{1,2,0:T(8,128)S(1)} all-gather(f32[1,96,32]{1,2,0:T(8,128)S(1)} %convolution_bitcast_fusion.3), channel_id=1, replica_groups=mesh['row'=4,'col'=8] {'row'}, dimensions={0}, use_global_device_ids=true | all-gather | bytes 61440 | tf_op jit(solution)/shard_map/all_gather | solution.py:73
  239.1 22.3 %psum.58 = f32[96,32]{0,1:T(8,128)S(1)} all-reduce(f32[96,32]{0,1:T(8,128)S(1)} %fusion.46), channel_id=1, replica_groups=mesh['row'=4,'col'=8] {'col'}, use_global_device_ids=true, to_apply=%region_5.8 | all-reduce | flops 3072 | bytes 24576 | tf_op jit(solution)/shard_map/psum | solution.py:60
  261.5 15.5 %psum.59 = f32[32,32]{0,1:T(8,128)S(1)} all-reduce(f32[32,32]{0,1:T(8,128)S(1)} %fusion.70), channel_id=1, replica_groups=mesh['row'=4,'col'=8] {'row'}, use_global_device_ids=true, to_apply=%region_6.9 | all-reduce | flops 1024 | bytes 8192 | tf_op jit(solution)/shard_map/psum | solution.py:68
  277.2 2.9 cholesky.85
  280.1 0.6 compare_reduce_fusion.2
  280.8 0.7 fusion.25
  281.4 2.4 custom-call.9
  283.8 0.2 convolution_bitcast_fusion.2
  284.1 13.1 %all-gather.1 = f32[4,96,32]{1,2,0:T(8,128)S(1)} all-gather(f32[1,96,32]{1,2,0:T(8,128)S(1)} %convolution_bitcast_fusion.2), channel_id=1, replica_groups=mesh['row'=4,'col'=8] {'row'}, dimensions={0}, use_global_device_ids=true | all-gather | bytes 61440 | tf_op jit(solution)/shard_map/all_gather | solution.py:73
  297.4 0.2 fusion.44
  297.6 22.3 %psum.60 = f32[96,32]{0,1:T(8,128)S(1)} all-reduce(f32[96,32]{0,1:T(8,128)S(1)} %fusion.44), channel_id=1, replica_groups=mesh['row'=4,'col'=8] {'col'}, use_global_device_ids=true, to_apply=%region_7.10 | all-reduce | flops 3072 | bytes 24576 | tf_op jit(solution)/shard_map/psum | solution.py:60
  320.1 16.3 %psum.61 = f32[32,32]{0,1:T(8,128)S(1)} all-reduce(f32[32,32]{0,1:T(8,128)S(1)} %fusion.71), channel_id=1, replica_groups=mesh['row'=4,'col'=8] {'row'}, use_global_device_ids=true, to_apply=%region_8.11 | all-reduce | flops 1024 | bytes 8192 | tf_op jit(solution)/shard_map/psum | solution.py:68
  336.5 2.9 cholesky.96
  339.4 0.6 compare_reduce_fusion.1
  340.1 0.7 fusion.26
  340.7 2.4 custom-call.10
  343.2 0.2 convolution_bitcast_fusion.1
  343.4 13.1 %all-gather.2 = f32[4,96,32]{1,2,0:T(8,128)S(1)} all-gather(f32[1,96,32]{1,2,0:T(8,128)S(1)} %convolution_bitcast_fusion.1), channel_id=1, replica_groups=mesh['row'=4,'col'=8] {'row'}, dimensions={0}, use_global_device_ids=true | all-gather | bytes 61440 | tf_op jit(solution)/shard_map/all_gather | solution.py:73
  356.7 0.2 fusion.42
  356.9 22.3 %psum.62 = f32[96,32]{0,1:T(8,128)S(1)} all-reduce(f32[96,32]{0,1:T(8,128)S(1)} %fusion.42), channel_id=1, replica_groups=mesh['row'=4,'col'=8] {'col'}, use_global_device_ids=true, to_apply=%region_9.12 | all-reduce | flops 3072 | bytes 24576 | tf_op jit(solution)/shard_map/psum | solution.py:60
  379.4 15.5 %psum.63 = f32[32,32]{0,1:T(8,128)S(1)} all-reduce(f32[32,32]{0,1:T(8,128)S(1)} %fusion.72), channel_id=1, replica_groups=mesh['row'=4,'col'=8] {'row'}, use_global_device_ids=true, to_apply=%region_10.13 | all-reduce | flops 1024 | bytes 8192 | tf_op jit(solution)/shard_map/psum | solution.py:68
  395.0 2.9 cholesky.107
  398.0 0.6 compare_reduce_fusion
  398.6 0.7 fusion.27
  399.3 2.4 custom-call.11
  401.7 0.2 convolution_bitcast_fusion
  402.0 13.1 %all-gather.3 = f32[4,96,32]{1,2,0:T(8,128)S(1)} all-gather(f32[1,96,32]{1,2,0:T(8,128)S(1)} %convolution_bitcast_fusion), channel_id=1, replica_groups=mesh['row'=4,'col'=8] {'row'}, dimensions={0}, use_global_device_ids=true | all-gather | bytes 61440 | tf_op jit(solution)/shard_map/all_gather | solution.py:73
  415.2 0.7 dynamic-slice_multiply_fusion
  (44 shorter events, 2.5 us)
Async XLA Ops:
  7.2 169.1 %copy-start = (f32[48,32]{0,1:T(8,128)S(1)}, f32[48,32]{0,1:T(8,128)}, u32[]{:S(2)}) copy-start(f32[48,32]{0,1:T(8,128)} %param.8) | copy-start | bytes 18436
  7.2 120.5 %all-gather.6.cloned.1.call-start = ((), (), s32[]{:S(2)}) async-start(), calls=%async_computation.1 | async-start | bytes 7864320 | tf_op jit(solution)/shard_map/all_gather | solution.py:45
  7.9 167.1 %reduce-scatter.4.cloned.1.call-start = ((), (), s32[]{:S(2)}) async-start(), calls=%async_computation.2 | async-start | bytes 663552
  9.6 4.0 copy-start.1
  131.8 6.0 %copy-start.2 = (f32[2,384,2048]{2,1,0:T(8,128)S(1)}, f32[2,384,2048]{2,1,0:T(8,128)}, u32[]{:S(2)}) copy-start(f32[2,384,2048]{2,1,0:T(8,128)} %all-gather.6.cloned.1.call-done) | copy-start | bytes 18874372
Sparse Core Ops, SparseCore 0:
  9.6 118.0 all-gather.5
  142.5 32.5 reduce-scatter.3
where the time goes:
time: 423 us
  blocking collectives  208 us (49%)
  waiting for transfers between devices  147 us (35%)
  other arithmetic  32.1 us (8%)
  matrix products  15.6 us (4%)
  between operations  14.4 us (3%)
  local copies, waits for them, and re-layouts  5.54 us (1%)
    all_gather x1, waiting for transfers between devices, local(): gathered = lax.all_gather(coefs, 'row', axis=1, tiled=True)  114 us
    psum x4, blocking collectives, local(): summed_rows = lax.psum(partial_value, 'col')  89.5 us
    psum x4, blocking collectives, local(): gram = lax.psum(local_gram, 'row')  66.1 us
    all_gather x4, blocking collectives, local(): whole = lax.all_gather(fresh, 'row', axis=0, tiled=True)  52.5 us
    unnamed x3, waiting for transfers between devices  33.4 us
    another operation x12, other arithmetic, local(): factor = jnp.linalg.cholesky(gram)  14.4 us
    dot_general x3, matrix products, inner(): lax.dot_general(left, right, (((1,), (1,)), ((), ())), precision=HIGH, pr...  13.2 us
    another operation x8, other arithmetic, local(): lax.linalg.triangular_solve(factor, summed_rows, left_side=False, lower=T...  12.3 us
  transfers between devices with their start and end apart: 2, of which 2 were waited for; matrix products, arithmetic and copies ran while one was open for 1% of the time, Pallas kernels for 0%

commit v1 on v0

--- a/solution.py
+++ b/solution.py
@@ -57,7 +57,7 @@
     current = start_basis
     for step in range(ITERS):
         partial_value = jnp.dot(block, current, precision=HIGH, preferred_element_type=jnp.float32)
-        summed_rows = lax.psum(partial_value, "col")
+        summed_rows = jnp.sum(lax.all_gather(partial_value, "col"), axis=0)
         local_gram = lax.dot_general(
             summed_rows,
             summed_rows,

time: 423 us -> 369 us (0.87)
  blocking collectives: 208 us -> 154 us
    psum x4 -> x0, blocking collectives: 89.5 us -> none  [local(): summed_rows = lax.psum(partial_value, 'col')]
    all_gather x0 -> x4, blocking collectives: none -> 34.9 us  [local(): summed_rows = jnp.sum(lax.all_gather(partial_value, 'col'), axis=0)]
  transfers between devices with their start and end apart: 2 -> 2, of which waited for: 2 -> 2; matrix products, arithmetic and copies ran while one was open for 1% -> 2% of each run, Pallas kernels for 0% -> 0%
where the time goes in v1:
time: 369 us; the launch traced here: 368 us
  blocking collectives  154 us (42%)
  waiting for transfers between devices  147 us (40%)
  other arithmetic  32.2 us (9%)
  matrix products  15.6 us (4%)
  between operations  14.4 us (4%)
  local copies, waits for them, and re-layouts  5.56 us (2%)
    all_gather x1, waiting for transfers between devices, local(): gathered = lax.all_gather(coefs, 'row', axis=1, tiled=True)  114 us
    psum x4, blocking collectives, local(): gram = lax.psum(local_gram, 'row')  66.3 us
    all_gather x4, blocking collectives, local(): whole = lax.all_gather(fresh, 'row', axis=0, tiled=True)  52.5 us
    all_gather x4, blocking collectives, local(): summed_rows = jnp.sum(lax.all_gather(partial_value, 'col'), axis=0)  34.9 us
    unnamed x3, waiting for transfers between devices  33.4 us
    another operation x12, other arithmetic, local(): factor = jnp.linalg.cholesky(gram)  14.4 us
    dot_general x3, matrix products, inner(): lax.dot_general(left, right, (((1,), (1,)), ((), ())), precision=HIGH, pr...  13.2 us
    another operation x8, other arithmetic, local(): lax.linalg.triangular_solve(factor, summed_rows, left_side=False, lower=T...  12.3 us
  transfers between devices with their start and end apart: 2, of which 2 were waited for; matrix products, arithmetic and copies ran while one was open for 2% of the time, Pallas kernels for 0%

profile of v1, /device:TPU:0, one launch (start us, length us, event | category | flops | bytes accessed | tf_op | source)
XLA Modules:
  0.0 368.4 jit_solution(15705106810537005991)
XLA Ops:
  7.2 0.7 all-gather.14.cloned.1.call-update
  8.0 0.8 constant_dynamic-slice_fusion
  8.8 0.8 slice_reduce_fusion.1
  9.6 4.0 %fusion.18 = f32[384,96]{0,1:T(8,128)S(1)} fusion(f32[2,96,2048]{2,1,0:T(8,128)} %param.6, s32[96]{0:T(128)S(1)} %get-tuple-element.20, s32[2048]{0:T(1024)S(1)} %get-tuple-element.22, s32[2048]{0:T(1024)S(1)} %get-tuple-element.21, s32[96]{0:T(128)S(1)} %get-tuple-element.19, s32[2048]{0:T(1024)S(1)} %broadcast_multiply_fusion, ...), kind=kOutput, calls=%fused_computation.32 | convolution fusion | flops 911671296 | bytes 1778688 | tf_op jit(solution)/shard_map/dot_general | solution.py:22
  13.6 0.4 bitcast_select_fusion.1
  14.0 113.6 %all-gather.14.cloned.1.call-done = f32[2,384,2048]{2,1,0:T(8,128)} async-done(((f32[2,96,2048]{2,1,0:T(8,128)}), f32[2,384,2048]{2,1,0:T(8,128)}) %all-gather.14.cloned.1.call-update) | async-done | bytes 6291472 | tf_op jit(solution)/shard_map/all_gather | solution.py:45
  127.6 4.1 %fusion.10 = (f32[384,2048]{1,0:T(8,128)S(1)}, f32[384,2048]{1,0:T(8,128)S(1)}) fusion(f32[2,384,2048]{2,1,0:T(8,128)} %all-gather.14.cloned.1.call-done, s32[384]{0:T(512)S(1)} %get-tuple-element.11, s32[2048]{0:T(1024)S(1)} %get-tuple-element.22, s32[2048]{0:T(1024)S(1)} %get-tuple-element.21, s32[384]{0:T(512)S(1)} %get-tuple-element.10, ...), kind=kLoop, calls=%fused_computation.14 | loop fusion | flops 5505024 | bytes 12612608 | tf_op jit(solution)/shard_map/mul | solution.py:29
  131.8 6.0 %fusion = f32[384,96]{0,1:T(8,128)S(1)} fusion(f32[384,2048]{1,0:T(8,128)S(1)} %get-tuple-element.13, f32[384,2048]{1,0:T(8,128)S(1)} %get-tuple-element.12, f32[96,2048]{1,0:T(8,128)S(1)} %get-tuple-element.15, f32[96,2048]{1,0:T(8,128)S(1)} %get-tuple-element.14), kind=kOutput, calls=%fused_computation | convolution fusion | flops 1813905408 | bytes 8011776 | tf_op jit(solution)/shard_map/dot_general | solution.py:22
  137.8 3.2 fusion.4
  141.1 1.2 copy.44
  142.3 32.7 %reduce-scatter.4.cloned.1.call-done = f32[48,288]{1,0:T(8,128)} async-done(((f32[384,288]{1,0:T(8,128)}), f32[48,288]{1,0:T(8,128)}) %reduce-scatter.4.cloned.1.call-update) | async-done | bytes 55312
  175.0 0.9 fusion.64
  176.5 0.7 copy.39
  177.2 9.1 %all-gather.4 = f32[8,96,32]{1,2,0:T(8,128)S(1)} all-gather(f32[1,96,32]{1,2,0:T(8,128)S(1)} %convolution_bitcast_fusion.7), channel_id=2, replica_groups=mesh['row'=4,'col'=8] {'col'}, dimensions={0}, use_global_device_ids=true | all-gather | bytes 110592 | tf_op jit(solution)/shard_map/all_gather | solution.py:60
  186.5 18.7 %psum.28 = f32[32,32]{0,1:T(8,128)S(1)} all-reduce(f32[32,32]{0,1:T(8,128)S(1)} %fusion.65), channel_id=1, replica_groups=mesh['row'=4,'col'=8] {'row'}, use_global_device_ids=true, to_apply=%region_2.3 | all-reduce | flops 1024 | bytes 8192 | tf_op jit(solution)/shard_map/psum | solution.py:68
  205.3 2.9 cholesky.74
  208.2 0.6 compare_reduce_fusion.3
  208.9 0.7 fusion.24
  209.6 2.4 custom-call.8
  212.0 0.2 convolution_bitcast_fusion.6
  212.2 13.1 %all-gather.5 = f32[4,96,32]{1,2,0:T(8,128)S(1)} all-gather(f32[1,96,32]{1,2,0:T(8,128)S(1)} %convolution_bitcast_fusion.6), channel_id=1, replica_groups=mesh['row'=4,'col'=8] {'row'}, dimensions={0}, use_global_device_ids=true | all-gather | bytes 61440 | tf_op jit(solution)/shard_map/all_gather | solution.py:73
  225.5 0.2 convolution_bitcast_fusion.5
  225.7 8.3 %all-gather.6 = f32[8,96,32]{1,2,0:T(8,128)S(1)} all-gather(f32[1,96,32]{1,2,0:T(8,128)S(1)} %convolution_bitcast_fusion.5), channel_id=3, replica_groups=mesh['row'=4,'col'=8] {'col'}, dimensions={0}, use_global_device_ids=true | all-gather | bytes 110592 | tf_op jit(solution)/shard_map/all_gather | solution.py:60
  234.2 15.5 %psum.29 = f32[32,32]{0,1:T(8,128)S(1)} all-reduce(f32[32,32]{0,1:T(8,128)S(1)} %fusion.66), channel_id=1, replica_groups=mesh['row'=4,'col'=8] {'row'}, use_global_device_ids=true, to_apply=%region_6.9 | all-reduce | flops 1024 | bytes 8192 | tf_op jit(solution)/shard_map/psum | solution.py:68
  249.8 2.9 cholesky.85
  252.7 0.6 compare_reduce_fusion.2
  253.4 0.7 fusion.25
  254.1 2.4 custom-call.9
  256.5 0.2 convolution_bitcast_fusion.4
  256.7 13.1 %all-gather.7 = f32[4,96,32]{1,2,0:T(8,128)S(1)} all-gather(f32[1,96,32]{1,2,0:T(8,128)S(1)} %convolution_bitcast_fusion.4), channel_id=1, replica_groups=mesh['row'=4,'col'=8] {'row'}, dimensions={0}, use_global_device_ids=true | all-gather | bytes 61440 | tf_op jit(solution)/shard_map/all_gather | solution.py:73
  270.0 0.2 convolution_bitcast_fusion.3
  270.2 9.2 %all-gather.8 = f32[8,96,32]{1,2,0:T(8,128)S(1)} all-gather(f32[1,96,32]{1,2,0:T(8,128)S(1)} %convolution_bitcast_fusion.3), channel_id=4, replica_groups=mesh['row'=4,'col'=8] {'col'}, dimensions={0}, use_global_device_ids=true | all-gather | bytes 110592 | tf_op jit(solution)/shard_map/all_gather | solution.py:60
  279.6 16.3 %psum.30 = f32[32,32]{0,1:T(8,128)S(1)} all-reduce(f32[32,32]{0,1:T(8,128)S(1)} %fusion.67), channel_id=1, replica_groups=mesh['row'=4,'col'=8] {'row'}, use_global_device_ids=true, to_apply=%region_8.11 | all-reduce | flops 1024 | bytes 8192 | tf_op jit(solution)/shard_map/psum | solution.py:68
  296.0 2.9 cholesky.96
  298.9 0.6 compare_reduce_fusion.1
  299.6 0.7 fusion.26
  300.2 2.4 custom-call.10
  302.7 0.2 convolution_bitcast_fusion.2
  302.9 13.1 %all-gather.9 = f32[4,96,32]{1,2,0:T(8,128)S(1)} all-gather(f32[1,96,32]{1,2,0:T(8,128)S(1)} %convolution_bitcast_fusion.2), channel_id=1, replica_groups=mesh['row'=4,'col'=8] {'row'}, dimensions={0}, use_global_device_ids=true | all-gather | bytes 61440 | tf_op jit(solution)/shard_map/all_gather | solution.py:73
  316.4 8.3 %all-gather.10 = f32[8,96,32]{1,2,0:T(8,128)S(1)} all-gather(f32[1,96,32]{1,2,0:T(8,128)S(1)} %convolution_bitcast_fusion.1), channel_id=5, replica_groups=mesh['row'=4,'col'=8] {'col'}, dimensions={0}, use_global_device_ids=true | all-gather | bytes 110592 | tf_op jit(solution)/shard_map/all_gather | solution.py:60
  324.9 15.7 %psum.31 = f32[32,32]{0,1:T(8,128)S(1)} all-reduce(f32[32,32]{0,1:T(8,128)S(1)} %fusion.68), channel_id=1, replica_groups=mesh['row'=4,'col'=8] {'row'}, use_global_device_ids=true, to_apply=%region_10.13 | all-reduce | flops 1024 | bytes 8192 | tf_op jit(solution)/shard_map/psum | solution.py:68
  340.6 2.9 cholesky.107
  343.6 0.6 compare_reduce_fusion
  344.2 0.7 fusion.27
  344.9 2.4 custom-call.11
  347.3 0.2 convolution_bitcast_fusion
  347.6 13.1 %all-gather.11 = f32[4,96,32]{1,2,0:T(8,128)S(1)} all-gather(f32[1,96,32]{1,2,0:T(8,128)S(1)} %convolution_bitcast_fusion), channel_id=1, replica_groups=mesh['row'=4,'col'=8] {'row'}, dimensions={0}, use_global_device_ids=true | all-gather | bytes 61440 | tf_op jit(solution)/shard_map/all_gather | solution.py:73
  360.8 0.7 dynamic-slice_multiply_fusion
  (48 shorter events, 2.5 us)
Async XLA Ops:
  7.2 169.1 %copy-start = (f32[48,32]{0,1:T(8,128)S(1)}, f32[48,32]{0,1:T(8,128)}, u32[]{:S(2)}) copy-start(f32[48,32]{0,1:T(8,128)} %param.8) | copy-start | bytes 18436
  7.2 120.5 %all-gather.14.cloned.1.call-start = ((), (), s32[]{:S(2)}) async-start(), calls=%async_computation.1 | async-start | bytes 7864320 | tf_op jit(solution)/shard_map/all_gather | solution.py:45
  7.9 167.1 %reduce-scatter.4.cloned.1.call-start = ((), (), s32[]{:S(2)}) async-start(), calls=%async_computation.2 | async-start | bytes 663552
  9.6 4.0 %copy-start.1 = (f32[2,96,2048]{2,1,0:T(8,128)S(1)}, f32[2,96,2048]{2,1,0:T(8,128)}, u32[]{:S(2)}) copy-start(f32[2,96,2048]{2,1,0:T(8,128)} %param.6) | copy-start | bytes 4718596
  131.8 6.0 %copy-start.2 = (f32[2,384,2048]{2,1,0:T(8,128)S(1)}, f32[2,384,2048]{2,1,0:T(8,128)}, u32[]{:S(2)}) copy-start(f32[2,384,2048]{2,1,0:T(8,128)} %all-gather.14.cloned.1.call-done) | copy-start | bytes 18874372
Sparse Core Ops, SparseCore 0:
  9.6 118.0 all-gather.13
  142.5 32.5 reduce-scatter.3
